TPU v7x, 32 devices: a whole 2x2x4 slice. The times are simulated.
32 devices in a mesh: groups: 2 (over y), dp: 4 (over z), tensor: 4 (over x, core).
Axes of the slice: x: 2, y: 2, z: 4, core: 2. Of those that a mesh axis runs over, the one named last changes fastest.
Arguments:
- patches: bfloat16 [8192, 1280], P(('groups', 'dp')), parts along dimension 0, may hold values from -64 to 64
- grids: int32 [8, 2], P(('groups', 'dp')), parts along dimension 0, may hold values from 16 to 32, as said below
- dest: int32 [8, 256], P(('groups', 'dp')), parts along dimension 0, may hold values from 0 to 1535, as said below
- norm_gain: float32 [1280], replicated, may hold values from 0.1 to 1.9
- qkv_weight: bfloat16 [3, 1280, 1280], P(None, None, 'tensor'), may hold values from -8 to 8
- qkv_bias: float32 [3, 1280], P(None, 'tensor'), may hold values from -3 to 3
- proj_weight: bfloat16 [1280, 1280], P('tensor'), may hold values from -0.15625 to 0.15625
- proj_bias: float32 [1280], replicated, may hold values from -3 to 3
- merge_gain: float32 [1280], replicated, may hold values from 0.1 to 1.9
- w_first: bfloat16 [5120, 5120], P('dp', 'tensor'), may hold values from -0.078125 to 0.078125
- b_first: float32 [5120], P('tensor'), may hold values from -3 to 3
- w_second: bfloat16 [5120, 8192], P('tensor', 'dp'), may hold values from -0.078125 to 0.078125
- b_second: float32 [8192], P('tensor'), may hold values from -3 to 3
- text_embed: bfloat16 [3072, 8192], P(('groups', 'dp'), 'tensor'), parts along dimension 0, may hold values from -6 to 6
Outputs:
- sequence: bfloat16 [3072, 8192], P(('groups', 'dp'), 'tensor'), parts along dimension 0
There are 2 independent parts, one for each index of `groups`. A program takes and returns all parts, laid end to end along the dimension named above; an argument that names none is the same for every part. Nothing has to cross between parts.
Inputs may be any that keep to these rules, and one draw needn't show every extreme that they name: `grids`: both sides of every grid are even, at least 16 and at most 32; in each part along `groups`, the first image (the one on dp index 0) has the full 32 x 32 grid. The rows dest[i, j] with j < grids[i, 0] * grids[i, 1] / 4 are distinct over all images; the live rows of one image reach at most 64 rows in each aligned block of 384 sequence rows, and exactly that many for a full grid.
All inputs are finite; a program needn't handle non-finite values.
Results may differ from a plain program's by a relative error of at most 0.014.
Values may be sent and summed in bfloat16 or wider, within the bound.
A program may use at most 128 MiB of HBM per device.

v0:
```python
import math
import jax
import jax.numpy as jnp
from jax import lax
from jax.sharding import PartitionSpec as P

HEAD_DIM = 80
PATCHES = 1024
MERGED = 256


def rms_scale(values, gain):
    return values * lax.rsqrt(jnp.mean(values * values, axis=-1, keepdims=True) + 1e-06) * gain


def local(
    patches,
    grids,
    dest,
    norm_gain,
    qkv_weight,
    qkv_bias,
    proj_weight,
    proj_bias,
    merge_gain,
    w_first,
    b_first,
    w_second,
    b_second,
    text_embed,
):
    rows_dev = patches.shape[0]
    images_dev = grids.shape[0]
    heads_dev = qkv_weight.shape[2] // HEAD_DIM
    live_count = grids[:, 0] * grids[:, 1]
    normed = rms_scale(patches.astype(jnp.float32), norm_gain).astype(jnp.bfloat16)
    projected = (
        jnp.einsum("rv,jvc->jrc", normed, qkv_weight, preferred_element_type=jnp.float32)
        + qkv_bias[:, None, :]
    )
    projected = projected.astype(jnp.bfloat16).reshape(3, images_dev, PATCHES, heads_dev, HEAD_DIM)
    scores = jnp.einsum(
        "iqhd,ikhd->ihqk", projected[0], projected[1], preferred_element_type=jnp.float32
    ) / math.sqrt(HEAD_DIM)
    live_keys = jnp.arange(PATCHES, dtype=jnp.int32)[None, :] < live_count[:, None]
    scores = jnp.where(live_keys[:, None, None, :], scores, jnp.float32(-1e30))
    peak_score = jnp.max(scores, axis=-1, keepdims=True)
    exponent = jnp.exp(scores - peak_score)
    weights = (exponent / jnp.sum(exponent, axis=-1, keepdims=True)).astype(jnp.bfloat16)
    attended = jnp.einsum(
        "ihqk,ikhd->iqhd", weights, projected[2], preferred_element_type=jnp.float32
    )
    attended = attended.astype(jnp.bfloat16).reshape(rows_dev, heads_dev * HEAD_DIM)
    partial_value = jnp.dot(attended, proj_weight, preferred_element_type=jnp.float32).astype(
        jnp.bfloat16
    )
    summed = lax.psum(partial_value, "tensor").astype(jnp.float32)
    resid = patches.astype(jnp.float32) + summed + proj_bias
    merged_in = rms_scale(resid, merge_gain).astype(jnp.bfloat16)
    merged_in = merged_in.reshape(rows_dev // 4, 4 * patches.shape[1])
    merged_dev = merged_in.shape[0]
    received = lax.all_to_all(merged_in, "dp", split_axis=1, concat_axis=0, tiled=True)
    first_out = lax.psum_scatter(
        jnp.dot(received, w_first, preferred_element_type=jnp.float32).astype(jnp.bfloat16),
        "dp",
        scatter_dimension=0,
        tiled=True,
    ).astype(jnp.float32)
    hidden = jax.nn.gelu(first_out + b_first, approximate=False).astype(jnp.bfloat16)
    second_rows = jnp.dot(
        hidden,
        lax.all_gather(w_second, "dp", axis=1, tiled=True),
        preferred_element_type=jnp.float32,
    ).astype(jnp.bfloat16)
    visual = lax.psum_scatter(second_rows, "tensor", scatter_dimension=1, tiled=True).astype(
        jnp.float32
    )
    visual = (visual + b_second).astype(jnp.bfloat16)
    feature_count = visual.shape[1]
    dp_count = lax.axis_size("dp")
    seq_rows = text_embed.shape[0]
    capacity = images_dev * (MERGED // dp_count)
    live_rows = (jnp.arange(MERGED, dtype=jnp.int32)[None, :] < (live_count // 4)[:, None]).reshape(
        merged_dev
    )
    dest_flat = dest.reshape(merged_dev)
    shard_id = jnp.where(live_rows, dest_flat // seq_rows, dp_count)
    local_row = dest_flat % seq_rows
    one_hot = (shard_id[:, None] == jnp.arange(dp_count, dtype=jnp.int32)[None, :]).astype(
        jnp.int32
    )
    before = jnp.cumsum(one_hot, axis=0) - one_hot
    slot_index = jnp.sum(before * one_hot, axis=1)
    buffer = (
        jnp.zeros((dp_count, capacity, feature_count), jnp.bfloat16)
        .at[shard_id, slot_index]
        .set(visual, mode="drop")
    )
    positions = (
        jnp.full((dp_count, capacity), seq_rows, jnp.int32)
        .at[shard_id, slot_index]
        .set(local_row, mode="drop")
    )
    arrived, arrived_rows = (
        lax.all_to_all(buffer, "dp", split_axis=0, concat_axis=0, tiled=True),
        lax.all_to_all(positions, "dp", split_axis=0, concat_axis=0, tiled=True),
    )
    sequence = text_embed.at[arrived_rows.reshape(-1)].set(
        arrived.reshape(-1, feature_count), mode="drop"
    )
    return sequence


def solution(mesh):
    in_specs = (
        P(("groups", "dp"), None),
        P(("groups", "dp"), None),
        P(("groups", "dp"), None),
        P(),
        P(None, None, "tensor"),
        P(None, "tensor"),
        P("tensor", None),
        P(),
        P(),
        P("dp", "tensor"),
        P("tensor"),
        P("tensor", "dp"),
        P("tensor"),
        P(("groups", "dp"), "tensor"),
    )
    out_specs = P(("groups", "dp"), "tensor")
    return jax.shard_map(local, mesh=mesh, in_specs=in_specs, out_specs=out_specs, check_vma=False)
```

profile of v0, /device:TPU:0, one launch (start us, length us, event | category | flops | bytes accessed | tf_op | source)
XLA Modules:
  0.0 749.1 jit_solution(11529100986900097305)
XLA Ops:
  6.5 2.9 copy.35
  9.4 0.7 fusion.104
  11.4 0.6 fusion.6
  12.0 1.1 copy-done.10
  13.1 2.9 fusion.15
  15.9 1.3 fusion.103
  17.3 10.9 %fusion.105 = (f32[4,1024]{1,0:T(4,128)S(1)}, f32[4,1024,1024]{1,2,0:T(8,128)}) fusion(pred[1024]{0:T(1024)(128)(4,1)S(1)} %iota_compare_fusion, bf16[1024,4,80]{0,2,1:T(8,128)(2,1)} %bitcast.76, bf16[1024,4,80]{0,2,1:T(8,128)(2,1)} %bitcast.75), kind=kOutput, calls=%fused_computation.150 | convolution fusion | flops 687866880 | bytes 18105344 | tf_op jit(solution)/shard_map/sub | solution.py:48
  28.1 7.6 %fusion.20 = bf16[4,80,1024]{2,1,0:T(8,128)(2,1)S(1)} fusion(bf16[1024,4,80]{0,2,1:T(8,128)(2,1)} %bitcast.74, f32[4,1024,1024]{1,2,0:T(8,128)} %get-tuple-element.17, f32[4,1024]{1,0:T(4,128)S(1)} %get-tuple-element.16), kind=kOutput, calls=%fused_computation.33 | convolution fusion | flops 679804928 | bytes 18104320 | tf_op jit(solution)/shard_map/ihqk,ikhd->iqhd/dot_general | solution.py:50
  35.8 3.1 convolution_convert_fusion.2
  39.1 62.5 %all-reduce.2.cloned.1.call-done = bf16[1024,1280]{1,0:T(8,128)(2,1)} async-done(((bf16[1024,1280]{1,0:T(8,128)(2,1)}), bf16[1024,1280]{1,0:T(8,128)(2,1)}) %all-reduce.2.cloned.1.call-update) | async-done | bytes 2621456 | tf_op jit(solution)/shard_map/psum | solution.py:57
  101.7 3.8 multiply_reduce_fusion
  105.8 2.6 multiply_convert_fusion
  108.4 5.6 all_to_all.25
  114.0 2.1 copy.26
  116.0 63.6 %all_to_all.33 = bf16[256,4,1280]{2,0,1:T(8,128)(2,1)S(1)} all-to-all(bf16[256,4,1280]{2,0,1:T(8,128)(2,1)S(1)} %copy.26), channel_id=1, replica_groups=mesh['groups'=2,'dp'=4,'tensor'=4] {'dp'}, dimensions={1} | all-to-all | bytes 5242880 | tf_op jit(solution)/shard_map/all_to_all | solution.py:62
  179.6 4.9 convolution_convert_fusion.1
  184.5 0.7 all-gather.2.cloned.1.call-update
  185.3 50.0 %reduce-scatter.3.cloned.1.call-done = bf16[256,1280]{1,0:T(8,128)(2,1)} async-done(((bf16[1024,1280]{1,0:T(8,128)(2,1)}), bf16[256,1280]{1,0:T(8,128)(2,1)}) %reduce-scatter.3.cloned.1.call-update) | async-done | bytes 655376 | tf_op jit(solution)/shard_map/reduce_scatter | solution.py:63
  235.3 358.0 %all-gather.2.cloned.1.call-done = bf16[1280,8192]{1,0:T(8,128)(2,1)} async-done(((bf16[1280,2048]{1,0:T(8,128)(2,1)}), bf16[1280,8192]{1,0:T(8,128)(2,1)}) %all-gather.2.cloned.1.call-update) | async-done | bytes 20971536 | tf_op jit(solution)/shard_map/all_gather | solution.py:72
  593.3 17.4 %convolution_convert_fusion = bf16[256,8192]{1,0:T(8,128)(2,1)} fusion(bf16[1280,8192]{1,0:T(8,128)(2,1)} %all-gather.2.cloned.1.call-done, bf16[256,1280]{1,0:T(8,128)(2,1)} %reduce-scatter.3.cloned.1.call-done, f32[1280]{0:T(1024)S(1)} %copy-done.13), kind=kOutput, calls=%fused_computation.8 | convolution fusion | flops 5392760832 | bytes 25826304 | tf_op jit(solution)/shard_map/dot_general | solution.py:70
  610.7 0.6 copy-done.6
  611.4 1.2 reduce-window.6
  613.1 0.6 broadcast_in_dim.23
  613.7 38.8 %scatter_fusion = s32[4,64]{1,0:T(4,128)} fusion(s32[4,64]{1,0:T(4,128)} %broadcast_in_dim.23, s32[256]{0:T(256)S(1)} %bitcast.71, s32[256]{0:T(256)S(1)} %get-tuple-element.10), kind=kCustom, calls=%fused_computation | custom fusion | bytes 5120 | tf_op jit(solution)/shard_map/scatter | solution.py:102
  652.5 3.2 all-to-all-start
  655.7 1.5 add_convert_fusion.1
  657.2 1.2 broadcast_in_dim.28
  658.4 48.1 %scatter_fusion.1 = bf16[4,64,2048]{2,1,0:T(8,128)(2,1)} fusion(bf16[4,64,2048]{2,1,0:T(8,128)(2,1)} %broadcast_in_dim.28, s32[256]{0:T(256)S(1)} %bitcast.72, bf16[256,2048]{1,0:T(8,128)(2,1)S(1)} %add_convert_fusion.1), kind=kCustom, calls=%fused_computation.1 | custom fusion | bytes 3147776 | tf_op jit(solution)/shard_map/scatter | solution.py:97
  706.5 5.0 all-to-all-start.2
  712.0 0.6 reduce.11
  712.8 24.2 %all-to-all-done.2 = bf16[4,64,2048]{2,1,0:T(8,128)(2,1)} async-done(((bf16[4,64,2048]{2,1,0:T(8,128)(2,1)}), bf16[4,64,2048]{2,1,0:T(8,128)(2,1)}, u32[]{:S(2)}, u32[]{:S(2)}) %all-to-all-start.2) | async-done | bytes 1048608 | tf_op jit(solution)/shard_map/all_to_all | solution.py:105
  736.9 5.7 scatter_fusion.2
  (56 shorter events, 1.9 us)
Async XLA Ops:
  6.5 173.1 %copy-start = (bf16[1280,1280]{1,0:T(8,128)(2,1)S(1)}, bf16[1280,1280]{1,0:T(8,128)(2,1)}, u32[]{:S(2)}) copy-start(bf16[1280,1280]{1,0:T(8,128)(2,1)} %param.23) | copy-start | bytes 9830404
  6.5 2.9 copy-start.9
  6.5 95.1 %all-reduce.2.cloned.1.call-start = ((), (), s32[]{:S(2)}) async-start(), calls=%async_computation.5 | async-start | bytes 5242880 | tf_op jit(solution)/shard_map/psum | solution.py:57
  6.5 4.8 copy-start.2
  11.4 1.7 copy-start.10
  11.4 1.7 copy-start.12
  11.4 1.7 copy-start.14
  28.1 7.6 %copy-start.11 = (bf16[320,1280]{1,0:T(8,128)(2,1)S(1)}, bf16[320,1280]{1,0:T(8,128)(2,1)}, u32[]{:S(2)}) copy-start(bf16[320,1280]{1,0:T(8,128)(2,1)} %param.20) | copy-start | bytes 2457604
  38.9 62.8 %copy-start.5 = (f32[1280]{0:T(1024)S(1)}, f32[1280]{0:T(1024)}, u32[]{:S(2)}) copy-start(f32[1280]{0:T(1024)} %param.21) | copy-start | bytes 15364
  38.9 66.6 %copy-start.7 = (f32[1280]{0:T(1024)S(1)}, f32[1280]{0:T(1024)}, u32[]{:S(2)}) copy-start(f32[1280]{0:T(1024)} %param.22) | copy-start | bytes 15364
  38.9 196.4 %reduce-scatter.3.cloned.1.call-start = ((), (), s32[]{:S(2)}) async-start(), calls=%async_computation.6 | async-start | bytes 3276800 | tf_op jit(solution)/shard_map/reduce_scatter | solution.py:63
  101.7 3.8 copy-start.3
  101.7 4.1 copy-start.4
  184.5 408.8 %copy-start.13 = (f32[1280]{0:T(1024)S(1)}, f32[1280]{0:T(1024)}, u32[]{:S(2)}) copy-start(f32[1280]{0:T(1024)} %param.24) | copy-start | bytes 15364
  184.5 408.8 %all-gather.2.cloned.1.call-start = ((), (), s32[]{:S(2)}) async-start(), calls=%async_computation.7 | async-start | bytes 26214400 | tf_op jit(solution)/shard_map/all_gather | solution.py:72
  185.2 470.5 %reduce-scatter.5.cloned.1.call-start = ((), (), s32[]{:S(2)}) async-start(), calls=%async_computation.8 | async-start | bytes 5242880 | tf_op jit(solution)/shard_map/reduce_scatter | solution.py:75
  610.7 0.7 copy-start.6
  610.7 45.0 %copy-start.8 = (f32[2048]{0:T(1024)S(1)}, f32[2048]{0:T(1024)}, u32[]{:S(2)}) copy-start(f32[2048]{0:T(1024)} %param.26) | copy-start | bytes 24580
  652.5 54.0 %all-to-all-start = ((s32[4,1,64]{2,1,0:T(1,128)}), s32[4,1,64]{2,1,0:T(1,128)S(1)}, u32[]{:S(2)}, u32[]{:S(2)}) async-start(s32[4,1,64]{2,1,0:T(1,128)} %bitcast.12), calls=%async_computation | async-start | bytes 4096 | tf_op jit(solution)/shard_map/all_to_all | solution.py:106
  706.5 30.4 %all-to-all-start.2 = ((bf16[4,64,2048]{2,1,0:T(8,128)(2,1)}), bf16[4,64,2048]{2,1,0:T(8,128)(2,1)}, u32[]{:S(2)}, u32[]{:S(2)}) async-start(bf16[4,64,2048]{2,1,0:T(8,128)(2,1)} %scatter_fusion.1), calls=%async_computation.4 | async-start | bytes 2097152 | tf_op jit(solution)/shard_map/all_to_all | solution.py:105
  736.9 5.7 copy-start.1
Sparse Core Ops, SparseCore 0:
  39.0 62.6 all-reduce.1
  184.6 50.6 reduce-scatter.2
  236.9 356.3 all-gather.1
  610.8 42.9 reduce-scatter.4
where the time goes:
time: 753 us; the launch traced here: 749 us
  waiting for transfers between devices  495 us (66%)
  local copies, waits for them, and re-layouts  110 us (15%)
  blocking collectives  63.6 us (8%)
  matrix products  46.7 us (6%)
  between operations  14.6 us (2%)
  other arithmetic  10.6 us (1%)
  starting transfers between devices  8.51 us (1%)
    all_gather x1, waiting for transfers between devices, local(): lax.all_gather(w_second, 'dp', axis=1, tiled=True)  358 us
    all_to_all x1, blocking collectives, local(): lax.all_to_all(merged_in, 'dp', split_axis=1, concat_axis=0, tiled=True)  63.6 us
    psum x1, waiting for transfers between devices, local(): summed = lax.psum(partial_value, 'tensor').astype(jnp.float32)  62.5 us
    reduce_scatter x1, waiting for transfers between devices, local(): lax.psum_scatter(jnp.dot(received, w_first, preferred_element_type=jnp.fl...  50 us
    scatter x1, local copies, waits for them, and re-layouts, local(): buffer = jnp.zeros((dp_count, capacity, feature_count), jnp.bfloat16).at[...  48.1 us
    scatter x1, local copies, waits for them, and re-layouts, local(): positions = jnp.full((dp_count, capacity), seq_rows, jnp.int32).at[shard_...  38.8 us
    all_to_all x1, waiting for transfers between devices, local(): lax.all_to_all(buffer, 'dp', split_axis=0, concat_axis=0, tiled=True)  24.2 us
    dot_general x1, matrix products, local(): jnp.dot(hidden, lax.all_gather(w_second, 'dp', axis=1, tiled=True), prefe...  17.4 us
  transfers between devices with their start and end apart: 6, of which 4 were waited for; matrix products, arithmetic and copies ran while one was open for 12% of the time, Pallas kernels for 0%

commit v1 on v0

--- a/solution.py
+++ b/solution.py
@@ -69,7 +69,7 @@
     hidden = jax.nn.gelu(first_out + b_first, approximate=False).astype(jnp.bfloat16)
     second_rows = jnp.dot(
         hidden,
-        lax.all_gather(w_second, "dp", axis=1, tiled=True),
+        jnp.concatenate(lax.all_gather(w_second, "dp"), axis=1),
         preferred_element_type=jnp.float32,
     ).astype(jnp.bfloat16)
     visual = lax.psum_scatter(second_rows, "tensor", scatter_dimension=1, tiled=True).astype(

time: 753 us -> 668 us (0.89)
  waiting for transfers between devices: 495 us -> 304 us
  blocking collectives: 63.6 us -> 143 us
  local copies, waits for them, and re-layouts: 110 us -> 136 us
    all_gather x1, waiting for transfers between devices: 358 us -> 192 us  [local(): lax.all_gather(w_second, 'dp')]
    all_to_all x1, blocking collectives: 63.6 us -> 143 us  [local(): lax.all_to_all(merged_in, 'dp', split_axis=1, concat_axis=0, tiled=True)]
    reshape x0 -> x1, local copies, waits for them, and re-layouts: none -> 27.7 us  [local(): jnp.concatenate(lax.all_gather(w_second, 'dp'), axis=1)]
    reduce_scatter x1, waiting for transfers between devices: 50 us -> 25.2 us  [local(): lax.psum_scatter(jnp.dot(received, w_first, preferred_element_type=jnp.fl...]
  transfers between devices with their start and end apart: 6 -> 6, of which waited for: 4 -> 4; matrix products, arithmetic and copies ran while one was open for 12% -> 20% of each run, Pallas kernels for 0% -> 0%
where the time goes in v1:
time: 668 us; the launch traced here: 664 us
  waiting for transfers between devices  304 us (46%)
  blocking collectives  143 us (21%)
  local copies, waits for them, and re-layouts  136 us (20%)
  matrix products  45.7 us (7%)
  between operations  16.4 us (2%)
  other arithmetic  10.6 us (2%)
  starting transfers between devices  8.54 us (1%)
    all_gather x1, waiting for transfers between devices, local(): lax.all_gather(w_second, 'dp')  192 us
    all_to_all x1, blocking collectives, local(): lax.all_to_all(merged_in, 'dp', split_axis=1, concat_axis=0, tiled=True)  143 us
    psum x1, waiting for transfers between devices, local(): summed = lax.psum(partial_value, 'tensor').astype(jnp.float32)  62 us
    scatter x1, local copies, waits for them, and re-layouts, local(): buffer = jnp.zeros((dp_count, capacity, feature_count), jnp.bfloat16).at[...  48.1 us
    scatter x1, local copies, waits for them, and re-layouts, local(): positions = jnp.full((dp_count, capacity), seq_rows, jnp.int32).at[shard_...  38.2 us
    reshape x1, local copies, waits for them, and re-layouts, local(): jnp.concatenate(lax.all_gather(w_second, 'dp'), axis=1)  27.7 us
    reduce_scatter x1, waiting for transfers between devices, local(): lax.psum_scatter(jnp.dot(received, w_first, preferred_element_type=jnp.fl...  25.2 us
    all_to_all x1, waiting for transfers between devices, local(): lax.all_to_all(buffer, 'dp', split_axis=0, concat_axis=0, tiled=True)  23.8 us
  transfers between devices with their start and end apart: 6, of which 4 were waited for; matrix products, arithmetic and copies ran while one was open for 20% of the time, Pallas kernels for 0%

profile of v1, /device:TPU:0, one launch (start us, length us, event | category | flops | bytes accessed | tf_op | source)
XLA Modules:
  0.0 664.0 jit_solution(1881379058950404054)
XLA Ops:
  7.4 2.9 copy.41
  10.3 0.7 fusion.104
  12.3 0.6 fusion.6
  12.9 2.9 fusion.15
  15.8 1.3 fusion.103
  17.1 10.9 %fusion.105 = (f32[4,1024]{1,0:T(4,128)S(1)}, f32[4,1024,1024]{1,2,0:T(8,128)}) fusion(pred[1024]{0:T(1024)(128)(4,1)S(1)} %iota_compare_fusion, bf16[1024,4,80]{0,2,1:T(8,128)(2,1)} %bitcast.85, bf16[1024,4,80]{0,2,1:T(8,128)(2,1)} %bitcast.84), kind=kOutput, calls=%fused_computation.150 | convolution fusion | flops 687866880 | bytes 18105344 | tf_op jit(solution)/shard_map/sub | solution.py:48
  28.0 7.6 %fusion.20 = bf16[4,80,1024]{2,1,0:T(8,128)(2,1)S(1)} fusion(bf16[1024,4,80]{0,2,1:T(8,128)(2,1)} %bitcast.83, f32[4,1024,1024]{1,2,0:T(8,128)} %get-tuple-element.17, f32[4,1024]{1,0:T(4,128)S(1)} %get-tuple-element.16), kind=kOutput, calls=%fused_computation.33 | convolution fusion | flops 679804928 | bytes 18104320 | tf_op jit(solution)/shard_map/ihqk,ikhd->iqhd/dot_general | solution.py:50
  35.7 3.1 convolution_convert_fusion.2
  38.8 0.5 all-gather.3.cloned.1.call-update
  39.6 62.0 %all-reduce.2.cloned.1.call-done = bf16[1024,1280]{1,0:T(8,128)(2,1)} async-done(((bf16[1024,1280]{1,0:T(8,128)(2,1)}), bf16[1024,1280]{1,0:T(8,128)(2,1)}) %all-reduce.2.cloned.1.call-update) | async-done | bytes 2621456 | tf_op jit(solution)/shard_map/psum | solution.py:57
  101.6 3.8 multiply_reduce_fusion
  105.7 2.7 multiply_convert_fusion
  108.3 5.6 all_to_all.25
  113.9 2.1 copy.31
  116.0 143.4 %all_to_all.33 = bf16[256,4,1280]{2,0,1:T(8,128)(2,1)S(1)} all-to-all(bf16[256,4,1280]{2,0,1:T(8,128)(2,1)S(1)} %copy.31), channel_id=1, replica_groups=mesh['groups'=2,'dp'=4,'tensor'=4] {'dp'}, dimensions={1} | all-to-all | bytes 5242880 | tf_op jit(solution)/shard_map/all_to_all | solution.py:62
  259.4 4.8 convolution_convert_fusion.1
  264.4 191.9 %all-gather.3.cloned.1.call-done = bf16[5120,2048]{1,0:T(8,128)(2,1)} async-done(((bf16[1280,2048]{1,0:T(8,128)(2,1)}), bf16[5120,2048]{1,0:T(8,128)(2,1)}) %all-gather.3.cloned.1.call-update) | async-done | bytes 20971536 | tf_op jit(solution)/shard_map/all_gather | solution.py:72
  456.3 27.7 %copy.32 = bf16[1280,4,2048]{0,2,1:T(8,128)(2,1)} copy(bf16[1280,4,2048]{2,0,1:T(8,128)(2,1)} %bitcast.80) | data formatting | bytes 41943040 | tf_op jit(solution)/shard_map/reshape | solution.py:72
  483.9 25.2 %reduce-scatter.3.cloned.1.call-done = bf16[256,1280]{1,0:T(8,128)(2,1)} async-done(((bf16[1024,1280]{1,0:T(8,128)(2,1)}), bf16[256,1280]{1,0:T(8,128)(2,1)}) %reduce-scatter.3.cloned.1.call-update) | async-done | bytes 655376 | tf_op jit(solution)/shard_map/reduce_scatter | solution.py:63
  509.2 16.4 %convolution_convert_fusion = bf16[256,8192]{1,0:T(8,128)(2,1)} fusion(bf16[1280,8192]{0,1:T(8,128)(2,1)} %bitcast.81, bf16[256,1280]{1,0:T(8,128)(2,1)} %reduce-scatter.3.cloned.1.call-done, f32[1280]{0:T(1024)S(1)} %copy-done.13), kind=kOutput, calls=%fused_computation.8 | convolution fusion | flops 5392760832 | bytes 25826304 | tf_op jit(solution)/shard_map/dot_general | solution.py:70
  525.7 0.6 copy-done.6
  526.4 1.2 reduce-window.6
  528.0 0.6 broadcast_in_dim.23
  528.6 38.2 %scatter_fusion = s32[4,64]{1,0:T(4,128)} fusion(s32[4,64]{1,0:T(4,128)} %broadcast_in_dim.23, s32[256]{0:T(256)S(1)} %bitcast.78, s32[256]{0:T(256)S(1)} %get-tuple-element.10), kind=kCustom, calls=%fused_computation | custom fusion | bytes 5120 | tf_op jit(solution)/shard_map/scatter | solution.py:102
  566.8 3.4 all-to-all-start
  570.3 1.5 add_convert_fusion.1
  571.8 1.2 broadcast_in_dim.28
  572.9 48.1 %scatter_fusion.1 = bf16[4,64,2048]{2,1,0:T(8,128)(2,1)} fusion(bf16[4,64,2048]{2,1,0:T(8,128)(2,1)} %broadcast_in_dim.28, s32[256]{0:T(256)S(1)} %bitcast.79, bf16[256,2048]{1,0:T(8,128)(2,1)S(1)} %add_convert_fusion.1), kind=kCustom, calls=%fused_computation.1 | custom fusion | bytes 3147776 | tf_op jit(solution)/shard_map/scatter | solution.py:97
  621.0 4.8 all-to-all-start.2
  626.4 0.6 reduce.11
  627.1 23.8 %all-to-all-done.2 = bf16[4,64,2048]{2,1,0:T(8,128)(2,1)} async-done(((bf16[4,64,2048]{2,1,0:T(8,128)(2,1)}), bf16[4,64,2048]{2,1,0:T(8,128)(2,1)}, u32[]{:S(2)}, u32[]{:S(2)}) %all-to-all-start.2) | async-done | bytes 1048608 | tf_op jit(solution)/shard_map/all_to_all | solution.py:105
  650.9 5.7 scatter_fusion.2
  (57 shorter events, 1.9 us)
Async XLA Ops:
  7.4 252.1 %copy-start = (bf16[1280,1280]{1,0:T(8,128)(2,1)S(1)}, bf16[1280,1280]{1,0:T(8,128)(2,1)}, u32[]{:S(2)}) copy-start(bf16[1280,1280]{1,0:T(8,128)(2,1)} %param.23) | copy-start | bytes 9830404
  7.4 2.9 copy-start.9
  7.4 94.2 %all-reduce.2.cloned.1.call-start = ((), (), s32[]{:S(2)}) async-start(), calls=%async_computation.5 | async-start | bytes 5242880 | tf_op jit(solution)/shard_map/psum | solution.py:57
  7.4 4.9 copy-start.2
  10.3 2.6 copy-start.10
  10.3 2.7 copy-start.12
  10.3 2.7 copy-start.14
  28.0 7.6 %copy-start.11 = (bf16[320,1280]{1,0:T(8,128)(2,1)S(1)}, bf16[320,1280]{1,0:T(8,128)(2,1)}, u32[]{:S(2)}) copy-start(bf16[320,1280]{1,0:T(8,128)(2,1)} %param.20) | copy-start | bytes 2457604
  38.8 62.8 %copy-start.5 = (f32[1280]{0:T(1024)S(1)}, f32[1280]{0:T(1024)}, u32[]{:S(2)}) copy-start(f32[1280]{0:T(1024)} %param.21) | copy-start | bytes 15364
  38.8 417.5 %all-gather.3.cloned.1.call-start = ((), (), s32[]{:S(2)}) async-start(), calls=%async_computation.8 | async-start | bytes 26214400 | tf_op jit(solution)/shard_map/all_gather | solution.py:72
  39.4 66.0 %copy-start.7 = (f32[1280]{0:T(1024)S(1)}, f32[1280]{0:T(1024)}, u32[]{:S(2)}) copy-start(f32[1280]{0:T(1024)} %param.22) | copy-start | bytes 15364
  39.4 469.8 %reduce-scatter.3.cloned.1.call-start = ((), (), s32[]{:S(2)}) async-start(), calls=%async_computation.6 | async-start | bytes 3276800 | tf_op jit(solution)/shard_map/reduce_scatter | solution.py:63
  101.6 3.8 copy-start.3
  101.6 4.1 copy-start.4
  264.3 305.9 %reduce-scatter.5.cloned.1.call-start = ((), (), s32[]{:S(2)}) async-start(), calls=%async_computation.7 | async-start | bytes 5242880 | tf_op jit(solution)/shard_map/reduce_scatter | solution.py:75
  456.3 52.9 %copy-start.13 = (f32[1280]{0:T(1024)S(1)}, f32[1280]{0:T(1024)}, u32[]{:S(2)}) copy-start(f32[1280]{0:T(1024)} %param.24) | copy-start | bytes 15364
  525.6 0.7 copy-start.6
  525.6 44.6 %copy-start.8 = (f32[2048]{0:T(1024)S(1)}, f32[2048]{0:T(1024)}, u32[]{:S(2)}) copy-start(f32[2048]{0:T(1024)} %param.26) | copy-start | bytes 24580
  566.8 54.2 %all-to-all-start = ((s32[4,1,64]{2,1,0:T(1,128)}), s32[4,1,64]{2,1,0:T(1,128)S(1)}, u32[]{:S(2)}, u32[]{:S(2)}) async-start(s32[4,1,64]{2,1,0:T(1,128)} %bitcast.12), calls=%async_computation | async-start | bytes 4096 | tf_op jit(solution)/shard_map/all_to_all | solution.py:106
  621.0 29.9 %all-to-all-start.2 = ((bf16[4,64,2048]{2,1,0:T(8,128)(2,1)}), bf16[4,64,2048]{2,1,0:T(8,128)(2,1)}, u32[]{:S(2)}, u32[]{:S(2)}) async-start(bf16[4,64,2048]{2,1,0:T(8,128)(2,1)} %scatter_fusion.1), calls=%async_computation.4 | async-start | bytes 2097152 | tf_op jit(solution)/shard_map/all_to_all | solution.py:105
  650.9 5.7 copy-start.1
Sparse Core Ops, SparseCore 0:
  38.9 62.6 all-reduce.1
  525.8 43.9 reduce-scatter.4
Sparse Core Ops, SparseCore 1:
  40.9 415.4 all-gather.2
  458.5 50.7 reduce-scatter.2
